TPU v7x, 32 devices: a whole 2x2x4 slice. The times are simulated.
32 devices in a mesh: dp: 2 (over x), ep: 16 (over z, y, core).
Axes of the slice: x: 2, y: 2, z: 4, core: 2. Of those that a mesh axis runs over, the one named last changes fastest.
Arguments:
- tokens: bfloat16 [4096, 2048], P(('dp', 'ep')), parts along dimension 0
- expert_ids: int32 [4096, 8], P(('dp', 'ep')), parts along dimension 0
- norm_gain: bfloat16 [2048], replicated
- w_router: bfloat16 [2048, 128], replicated
- w_gate: bfloat16 [128, 2048, 768], P('ep')
- w_up: bfloat16 [128, 2048, 768], P('ep')
- w_down: bfloat16 [128, 768, 2048], P('ep')
Outputs:
- output: bfloat16 [4096, 2048], P(('dp', 'ep')), parts along dimension 0
There are 2 independent parts. A program takes and returns all parts, laid end to end along the dimension named above; an argument that names none is the same for every part.
All inputs are finite; a program needn't handle non-finite values.
Results may differ from a plain program's by a relative error of at most 0.00575139.
Values are sent between devices in bfloat16 or wider.
A program may use at most 1 GiB of HBM per device.

v0:
```python
import functools

import jax
import jax.numpy as jnp
from jax import lax
from jax.experimental import pallas as pl
from jax.experimental.pallas import tpu as pltpu
from jax.sharding import PartitionSpec as P

NORM_EPS = 1e-5
LANES = 128
BM = 128
WIN = 256
CUTS = 1
TILE = 16
PITCH = 17
STEP = 8
MORE = 8
PIECES = 4
QUAD = 4
PLANES = 4
F32 = jnp.float32
BF16 = jnp.bfloat16


def iota(shape, dim):
    return lax.broadcasted_iota(jnp.int32, shape, dim)


def place():
    me = lax.axis_index('ep')
    return me, me // QUAD, lax.rem(me, QUAD)


def remote(src, dst, send, recv, dev):
    return pltpu.make_async_remote_copy(src_ref=src, dst_ref=dst, send_sem=send, recv_sem=recv,
                                        device_id={'ep': dev}, device_id_type=pl.DeviceIdType.MESH)


def spread_kernel(r_max, x_ref, ids_ref, gain_ref, wr_ref, u_hbm, meta_hbm, ints_hbm,
                  u_all, xs, ub, pos_s, p_s, packet, meta, ints,
                  send_u, recv_u, send_m, recv_m, out_sem):
    n_dev = PLANES * QUAD
    me, z, q = place()
    y, c = q // 2, lax.rem(q, 2)
    half = u_all.shape[1] // 2
    tok = x_ref.shape[0]
    sub = u_all.shape[1] // tok

    barrier = pltpu.get_barrier_semaphore()
    for d in range(1, n_dev):
        pl.semaphore_signal(barrier, inc=1, device_id={'ep': lax.rem(me + d, n_dev)}, device_id_type=pl.DeviceIdType.MESH)

    x32 = x_ref[...].astype(F32)
    inv = lax.rsqrt(jnp.mean(x32 * x32, axis=1, keepdims=True) + NORM_EPS)
    ub[...] = (x32 * inv * gain_ref[...].astype(F32)).astype(BF16)
    for j in range(sub):
        xs[pl.ds(j, tok, stride=sub), :] = ub[:, j * LANES:(j + 1) * LANES].astype(F32)
    u_all[me] = xs[...].astype(BF16)
    pl.semaphore_wait(barrier, n_dev - 1)

    dest = (me + QUAD, me - QUAD, z * QUAD + (1 - y) * 2 + c, z * QUAD + y * 2 + 1 - c)

    def hop(b, h, way):
        rows = u_all.at[b, pl.ds(h * half, half)]
        return remote(rows, rows, send_u.at[b, h, way], recv_u.at[b, h], dest[way])

    def out_copy(b, h):
        rows = pl.ds(h * half, half)
        return pltpu.make_async_copy(u_all.at[b, rows], u_hbm.at[b, rows], out_sem.at[b, h])

    for h in range(2):
        @pl.when(z < PLANES - 1)
        def _():
            hop(me, h, 0).start()

        @pl.when(z > 0)
        def _():
            hop(me, h, 1).start()

        hop(me, h, 2).start()
        hop(me, h, 3).start()
        out_copy(me, h).start()

    logits = jnp.dot(ub[...], wr_ref[...], preferred_element_type=F32)
    top = jnp.max(logits, axis=1, keepdims=True)
    ex = jnp.exp(logits - top)
    p_s[...] = ex / jnp.sum(ex, axis=1, keepdims=True)
    lane = iota((tok, LANES), 1)
    hit = lane < 0
    ids = ids_ref[...].T
    for k in range(ids.shape[1]):
        hit = jnp.logical_or(hit, ids[:, k:k + 1] == lane)
    hit32 = hit.astype(F32)
    hit_b = hit32.astype(BF16)
    tri = (iota((tok, tok), 0) > iota((tok, tok), 1)).astype(F32).astype(BF16)
    rank = jnp.dot(tri, hit_b, preferred_element_type=F32)
    count = jnp.sum(hit32, axis=0, keepdims=True)
    row_e, col_e = iota((LANES, LANES), 0), iota((LANES, LANES), 1)
    e_loc = LANES // n_dev
    before = jnp.logical_and(row_e < col_e, row_e // e_loc == col_e // e_loc).astype(F32).astype(BF16)
    count8 = jnp.broadcast_to(count, (8, LANES))
    base = jnp.dot(count8.astype(BF16), before, preferred_element_type=F32)[0:1]
    pos_s[...] = jnp.where(hit, base + rank, -1.0)
    t_id = iota((tok, LANES), 0).astype(F32)
    lane_f = lane.astype(F32)

    def pack(zd, _):
        for m in range(QUAD):
            tk = jnp.zeros((tok, LANES), F32)
            gt = jnp.zeros((tok, LANES), F32)
            for ee in range(e_loc):
                col = m * e_loc + ee
                at = pos_s[:, col:col + 1] == lane_f
                tk = jnp.where(at, t_id, tk)
                gt = jnp.where(at, p_s[:, col:col + 1], gt)
            packet[zd, m:m + 1, :] = jnp.sum(tk, axis=0, keepdims=True)
            packet[zd, QUAD + m:QUAD + m + 1, :] = jnp.sum(gt, axis=0, keepdims=True)
        packet[zd, 8:16, :] = count8
        pos_s[...] = pltpu.roll(pos_s[...], LANES - QUAD * e_loc, 1)
        p_s[...] = pltpu.roll(p_s[...], LANES - QUAD * e_loc, 1)
        return 0

    lax.fori_loop(0, PLANES, pack, 0)

    def route_copy(d):
        return remote(packet.at[d // QUAD], meta.at[me], send_m.at[d], recv_m.at[me], d)

    for d in range(n_dev):
        @pl.when(d != me)
        def _():
            route_copy(d).start()

    meta[me] = packet[z]

    def take(b, h, ways):
        hop(b, h, 3).wait_recv()
        out_copy(b, h).start()
        for way in ways:
            hop(b, h, way).start()

    def from_z(d, fn):
        @pl.when(z >= d)
        def _():
            fn(me - QUAD * d, 0, z < PLANES - 1)

        @pl.when(z + d < PLANES)
        def _():
            fn(me + QUAD * d, 1, z > 0)

    def across(zb):
        return zb * QUAD + (1 - y) * 2 + c

    def step_z(d):
        for h in range(2):
            def on(b, way, more):
                hop(b, h, 3).wait_recv()

                @pl.when(more)
                def _():
                    hop(b, h, way).start()

                hop(b, h, 2).start()
                hop(b, h, 3).start()
                out_copy(b, h).start()

            from_z(d, on)

    def step_y(d):
        for h in range(2):
            if d == 0:
                take(across(z), h, (3,))
            else:
                @pl.when(z >= d)
                def _():
                    take(across(z - d), h, (3,))

                @pl.when(z + d < PLANES)
                def _():
                    take(across(z + d), h, (3,))

    step_z(1)
    step_y(0)
    step_z(2)
    step_y(1)
    step_z(3)
    step_y(2)
    step_y(3)
    for b in range(n_dev):
        @pl.when(b % 2 != c)
        def _():
            for h in range(2):
                hop(b, h, 3).wait_recv()
                out_copy(b, h).start()

    for d in range(n_dev):
        @pl.when(d != me)
        def _():
            remote(packet.at[0], meta.at[d], send_m.at[d], recv_m.at[d], d).wait_recv()

    cnt = meta[:, 8, :]
    group = (iota((LANES, LANES), 0) // e_loc == iota((LANES, LANES), 1)).astype(F32).astype(BF16)
    n_rows = jnp.dot(cnt.astype(BF16), group, preferred_element_type=F32)
    ints[0:16, LANES:] = jnp.zeros((16, LANES), jnp.int32)
    ints[0:16, :LANES] = meta[:, pl.ds(q, 1), :].reshape(n_dev, LANES).astype(jnp.int32)
    ints[16:32, :LANES] = cnt.astype(jnp.int32)
    run = jnp.zeros((1, LANES), F32)
    for s in range(n_dev):
        off = run.astype(jnp.int32)
        ints[32 + s:33 + s, :LANES] = off
        ints[48 + s:49 + s, :LANES] = jnp.minimum(off // TILE, (r_max - WIN) // TILE)
        run = run + n_rows[s:s + 1]

    tail = [pltpu.make_async_copy(meta, meta_hbm, out_sem.at[0, 2]), pltpu.make_async_copy(ints, ints_hbm, out_sem.at[1, 2])]
    for cp in tail:
        cp.start()

    for h in range(2):
        def sent(b, way, more):
            @pl.when(more)
            def _():
                hop(b, h, way).wait_send()

            hop(b, h, 2).wait_send()
            hop(b, h, 3).wait_send()

        @pl.when(z < PLANES - 1)
        def _():
            hop(me, h, 0).wait_send()

        @pl.when(z > 0)
        def _():
            hop(me, h, 1).wait_send()

        hop(me, h, 2).wait_send()
        hop(me, h, 3).wait_send()
        for d in range(1, PLANES):
            from_z(d, sent)
        for zb in range(PLANES):
            hop(across(zb), h, 3).wait_send()
        for b in range(n_dev):
            out_copy(b, h).wait()
    for d in range(n_dev):
        @pl.when(d != me)
        def _():
            route_copy(d).wait_send()
    for cp in tail:
        cp.wait()


def spread(r_max, tokens, expert_ids, norm_gain, w_router):
    tok, width = tokens.shape
    n_dev = PLANES * QUAD
    sub = width // LANES
    hbm = pl.BlockSpec(memory_space=pltpu.HBM)
    vmem = pl.BlockSpec(memory_space=pltpu.VMEM)
    return pl.pallas_call(
        functools.partial(spread_kernel, r_max),
        out_shape=(jax.ShapeDtypeStruct((n_dev, tok * sub, LANES), BF16),
                   jax.ShapeDtypeStruct((n_dev, 16, LANES), F32),
                   jax.ShapeDtypeStruct((64, 2 * LANES), jnp.int32)),
        in_specs=[vmem] * 4,
        out_specs=(hbm, hbm, hbm),
        scratch_shapes=[
            pltpu.VMEM((n_dev, tok * sub, LANES), BF16),
            pltpu.VMEM((tok * sub, LANES), F32),
            pltpu.VMEM((tok, width), BF16),
            pltpu.VMEM((tok, LANES), F32),
            pltpu.VMEM((tok, LANES), F32),
            pltpu.VMEM((PLANES, 16, LANES), F32),
            pltpu.VMEM((n_dev, 16, LANES), F32),
            pltpu.VMEM((64, 2 * LANES), jnp.int32),
            pltpu.SemaphoreType.DMA((n_dev, 2, 4)),
            pltpu.SemaphoreType.DMA((n_dev, 2)),
            pltpu.SemaphoreType.DMA((n_dev,)),
            pltpu.SemaphoreType.DMA((n_dev,)),
            pltpu.SemaphoreType.DMA((n_dev, 3)),
        ],
        compiler_params=pltpu.CompilerParams(collective_id=0, has_side_effects=True, vmem_limit_bytes=66_000_000),
        name="spread",
    )(tokens, expert_ids.T, norm_gain.reshape(1, width), w_router)


def expert_kernel(n_src, sub, r_max, ints, meta, u_hbm, w1_hbm, w3_hbm, w2_hbm, o_hbm, win_hbm,
                  u_vm, o_all, xf, xb, hb, ob, win, w1, w3, w2, pre, sems, sem_w):
    n_exp = w1_hbm.shape[0]
    me, z, q = place()
    lane0 = me * n_exp

    def load(e, names):
        slot = lax.rem(e, 2)
        copies = []
        for i, (src, dst) in enumerate(((w1_hbm, w1), (w3_hbm, w3), (w2_hbm, w2))):
            if i in names:
                size = src.shape[1] // PIECES
                for p in range(PIECES):
                    part = pl.ds(p * size, size)
                    copies.append(pltpu.make_async_copy(src.at[e, part], dst.at[slot, part], sem_w.at[slot, i, p]))
        return copies

    def start(copies):
        for i, w in enumerate(copies):
            w.start(priority=i % 2)

    def begin():
        cp = pltpu.make_async_copy(u_hbm, u_vm, sems.at[0])
        cp.start()
        for e in range(2):
            start(load(e, (0, 1, 2)))
        for s in range(n_src):
            pre[s] = 0

        @pl.loop(0, r_max * PITCH // 256)
        def _(i):
            o_all[pl.ds(pl.multiple_of(i * 256, 256), 256), :] = jnp.zeros((256, LANES), F32)

        @pl.loop(0, n_src)
        def _(s):
            for m in range(QUAD):
                t = meta[s, m:m + 1, :]
                g = meta[s, QUAD + m:QUAD + m + 1, :]
                hi = g.astype(BF16).astype(F32)
                mid = (g - hi).astype(BF16).astype(F32)
                lo = (g - hi - mid).astype(BF16).astype(F32)
                rows = jnp.concatenate([t, hi, mid, lo, t, t, t, t], axis=0)
                rows = jnp.concatenate([rows, jnp.zeros((8, WIN - LANES), F32)], axis=1)
                r = z * QUAD + m
                win[s * QUAD + m] = pltpu.roll(rows, ints[32 + s, r] - TILE * ints[48 + s, r], 1)

        pltpu.make_async_copy(win, win_hbm, sems.at[1]).start()
        cp.wait()

    begin()

    def expert(e, _):
        slot = lax.rem(e, 2)
        def take(s, j0, n, i, at):
            t = s * LANES + ints[s, j0 + i]
            src = u_vm[pl.ds(pl.multiple_of(t * sub, sub), sub), :]
            xf[pl.ds(at * PITCH, sub), :] = src.astype(F32)

        def give(s, j0, n, i, at):
            o_all[pl.ds(at * PITCH, sub), :] = xf[pl.ds((n + i) * PITCH, sub), :]

        def sweep(body, target, spare):
            n = jnp.int32(0)
            top = jnp.int32(0)
            starts = []
            for s in range(n_src):
                cnt = ints[16 + s, lane0 + e]
                to = target(s, n)
                for i in range(STEP):
                    at = to + i if target is by_row else jnp.where(i < cnt, to + i, spare)
                    body(s, pre[s], n, i, at)
                starts.append(n)
                n = n + cnt
                top = jnp.maximum(top, cnt)
            for s in range(n_src):
                cnt = ints[16 + s, lane0 + e]

                @pl.when(cnt > STEP)
                def _():
                    to = target(s, starts[s])
                    for i in range(STEP, STEP + MORE):
                        body(s, pre[s], starts[s], i, jnp.where(i < cnt, to + i, spare))

            @pl.when(top > STEP + MORE)
            def _():
                def source(s, n):
                    cnt = ints[16 + s, lane0 + e]

                    def row(i, _):
                        body(s, pre[s], n, i, target(s, n) + i)
                        return 0

                    lax.fori_loop(STEP + MORE, cnt, row, 0)
                    return n + cnt

                lax.fori_loop(0, n_src, source, jnp.int32(0))

            return n

        def by_row(s, n):
            return n

        def by_slot(s, n):
            return ints[32 + s, me] + pre[s]

        n = sweep(take, by_row, r_max + 2 * STEP)

        for w in load(e, (0, 1, 2)):
            w.wait()

        def block(b, _):
            r0 = b * (BM * PITCH)
            for j in range(sub):
                xb[:, j * LANES:(j + 1) * LANES] = xf[pl.ds(r0 + j, BM, stride=PITCH), :].astype(BF16)
            g = jnp.dot(xb[...], w1[slot], preferred_element_type=F32)
            v = jnp.dot(xb[...], w3[slot], preferred_element_type=F32)
            hb[...] = (jax.nn.silu(g) * v).astype(BF16)
            for k in range(sub // 4):
                o = jnp.dot(hb[...], w2[slot, :, k * 512:(k + 1) * 512], preferred_element_type=F32)
                for j in range(4):
                    xf[pl.ds(r0 + k * 4 + j, BM, stride=PITCH), :] = o[:, j * LANES:(j + 1) * LANES]
            return 0

        lax.fori_loop(0, (n + BM - 1) // BM, block, 0)

        sweep(give, by_slot, r_max)
        for s in range(n_src):
            pre[s] = pre[s] + ints[16 + s, lane0 + e]

        @pl.when(e + 2 < n_exp)
        def _():
            start(load(e + 2, (0, 1, 2)))

        return 0

    lax.fori_loop(0, n_exp, expert, 0)

    def put(j):
        return pltpu.make_async_copy(ob.at[j % 4], o_hbm.at[j], sems.at[2 + j % 4])

    for j in range(sub):
        if j >= 4:
            put(j - 4).wait()
        ob[j % 4] = o_all[pl.ds(j, r_max, stride=PITCH), :].astype(BF16)
        put(j).start()
    for j in range(sub - 4, sub):
        put(j).wait()
    pltpu.make_async_copy(win, win_hbm, sems.at[1]).wait()


def experts(n_src, r_max, ints, meta, u_rows, w1, w3, w2):
    n_exp, width, ff = w1.shape
    sub = width // LANES
    n_tok = u_rows.shape[0] // sub
    hbm = pl.BlockSpec(memory_space=pltpu.HBM)
    smem = pl.BlockSpec(memory_space=pltpu.SMEM)
    return pl.pallas_call(
        functools.partial(expert_kernel, n_src, sub, r_max),
        out_shape=(jax.ShapeDtypeStruct((sub, r_max, LANES), BF16),
                   jax.ShapeDtypeStruct((n_src * QUAD, 8, WIN), F32)),
        in_specs=[smem, pl.BlockSpec(memory_space=pltpu.VMEM), hbm, hbm, hbm, hbm],
        out_specs=(hbm, hbm),
        scratch_shapes=[
            pltpu.VMEM((n_tok * sub, LANES), BF16),
            pltpu.VMEM(((r_max + 8) * PITCH, LANES), F32),
            pltpu.VMEM(((r_max + 2 * STEP + 8) * PITCH, LANES), F32),
            pltpu.VMEM((BM, width), BF16),
            pltpu.VMEM((BM, ff), BF16),
            pltpu.VMEM((4, r_max, LANES), BF16),
            pltpu.VMEM((n_src * QUAD, 8, WIN), F32),
            pltpu.VMEM((2, width, ff), BF16),
            pltpu.VMEM((2, width, ff), BF16),
            pltpu.VMEM((2, ff, width), BF16),
            pltpu.SMEM((n_src,), jnp.int32),
            pltpu.SemaphoreType.DMA((6,)),
            pltpu.SemaphoreType.DMA((2, 3, PIECES)),
        ],
        compiler_params=pltpu.CompilerParams(vmem_limit_bytes=66_000_000),
        name="experts",
    )(ints, meta, u_rows, w1, w3, w2)


def collect_kernel(n_src, steps, ints, win, x_ref, o_hbm, out_ref,
                   mix, part, from_l, from_r, fin,
                   send_q, recv_q, send_z, recv_l, recv_r, send_f, recv_f, stage, stage_sem, *rows):
    me, z, q = place()
    y, c = q // 2, lax.rem(q, 2)
    tok = x_ref.shape[0]
    plane = QUAD * tok
    others = ((1 - y) * 2 + c, (1 - y) * 2 + 1 - c, y * 2 + 1 - c)

    barrier = pltpu.get_barrier_semaphore()

    def hello(dev):
        pl.semaphore_signal(barrier, inc=1, device_id={'ep': dev}, device_id_type=pl.DeviceIdType.MESH)

    def stage_copy(k, m):
        return pltpu.make_async_copy(o_hbm.at[m * steps + k], stage.at[k, m], stage_sem.at[k, m])

    def own_copy(k):
        return pltpu.make_async_copy(o_hbm.at[q * steps + k], rows[k].at[q], recv_q.at[k, q])

    for k in range(steps):
        for m in others:
            stage_copy(k, m).start()
        own_copy(k).start()

    for m in others:
        hello(z * QUAD + m)

    @pl.when(z > 0)
    def _():
        hello(me - QUAD)

    @pl.when(z < PLANES - 1)
    def _():
        hello(me + QUAD)

    pl.semaphore_wait(barrier, 4 + (z + PLANES - 1) // PLANES - (z + 1) // PLANES)

    def quad_copy(k, m):
        return remote(stage.at[k, m], rows[k].at[q], send_q.at[k, m], recv_q.at[k, q], z * QUAD + m)

    def quad_wait(k, m):
        remote(stage.at[k, m], rows[k].at[m], send_q.at[k, m], recv_q.at[k, m], z * QUAD + m).wait_recv()

    for k in range(steps):
        for m in others:
            stage_copy(k, m).wait()
            quad_copy(k, m).start()

    row_id = iota((tok, WIN), 0).astype(F32)

    def build(i, _):
        w = win[i]
        at = w[0:1] == row_id
        for part_i in range(3):
            mix[i, part_i * tok:(part_i + 1) * tok, :] = jnp.where(at, w[1 + part_i:2 + part_i], 0.0).astype(BF16)
        return 0

    lax.fori_loop(0, n_src * QUAD, build, 0)

    def combine(k):
        own_copy(k).wait()
        for m in others:
            quad_wait(k, m)

        def token_block(s, _):
            acc = jnp.zeros((3 * tok, LANES), F32)
            for m in range(QUAD):
                start = ints[48 + s, z * QUAD + m]
                span = jnp.concatenate([rows[k][m, start + i] for i in range(WIN // TILE)], axis=0)
                acc += jnp.dot(mix[s * QUAD + m], span, preferred_element_type=F32)
            part[k, s // QUAD, pl.ds(pl.multiple_of(lax.rem(s, QUAD) * tok, tok), tok), :] = acc[0:tok] + acc[tok:2 * tok] + acc[2 * tok:]

            return 0

        lax.fori_loop(0, n_src, token_block, 0)

    bit = plane // CUTS

    def right(k, zd, h):
        part_h = pl.ds(h * bit, bit)
        return remote(part.at[k, zd, part_h], from_l.at[k, zd, part_h], send_z.at[k, zd, h], recv_l.at[k, zd, h], me + QUAD)

    def left(k, zd, h):
        part_h = pl.ds(h * bit, bit)
        return remote(part.at[k, zd, part_h], from_r.at[k, zd, part_h], send_z.at[k, zd, h], recv_r.at[k, zd, h], me - QUAD)

    def forward(k):
        for i, h in [(i, h) for i in range(PLANES - 1) for h in range(CUTS)]:
            for to_right in (True, False):
                zd = PLANES - 1 - i if to_right else i
                box = from_l if to_right else from_r
                go = right if to_right else left
                rows_h = pl.ds(h * bit, bit)

                @pl.when(z < zd if to_right else z > zd)
                def _():
                    @pl.when(z > 0 if to_right else z < PLANES - 1)
                    def _():
                        go(k, zd, h).wait_recv()
                        part[k, zd, rows_h] += box[k, zd, rows_h]

                    go(k, zd, h).start()

    def final_copy(k, m):
        src = part.at[k, z, pl.ds(m * tok, tok)]
        return remote(src, fin.at[k, q], send_f.at[k, m], recv_f.at[k, q], z * QUAD + m)

    def finish(k):
        @pl.when(z > 0)
        def _():
            for h in range(CUTS):
                right(k, z, h).wait_recv()
            part[k, z] += from_l[k, z]

        @pl.when(z < PLANES - 1)
        def _():
            for h in range(CUTS):
                left(k, z, h).wait_recv()
            part[k, z] += from_r[k, z]

        for m in others:
            final_copy(k, m).start()
        fin[k, q] = part[k, z, pl.ds(pl.multiple_of(q * tok, tok), tok), :]

    for k in range(steps):
        combine(k)
        forward(k)
        if k > 0:
            finish(k - 1)
    finish(steps - 1)

    for k in range(steps):
        for m in others:
            remote(part.at[k, z, pl.ds(0, tok)], fin.at[k, m], send_f.at[k, m], recv_f.at[k, m], z * QUAD + m).wait_recv()
        for m in range(QUAD):
            cols = pl.ds((m * steps + k) * LANES, LANES)
            out_ref[:, cols] = (x_ref[:, cols].astype(F32) + fin[k, m]).astype(BF16)

    for k in range(steps):
        for m in others:
            quad_copy(k, m).wait_send()
            final_copy(k, m).wait_send()
        for zd in range(PLANES):
            @pl.when(z < zd)
            def _():
                for h in range(CUTS):
                    right(k, zd, h).wait_send()

            @pl.when(z > zd)
            def _():
                for h in range(CUTS):
                    left(k, zd, h).wait_send()


def collect(ints, win, tokens, o_rows):
    tok, width = tokens.shape
    sub, r_tiles = o_rows.shape[:2]
    n_src = PLANES * QUAD
    steps = sub // QUAD
    vmem = pl.BlockSpec(memory_space=pltpu.VMEM)
    return pl.pallas_call(
        functools.partial(collect_kernel, n_src, steps),
        out_shape=jax.ShapeDtypeStruct((tok, width), BF16),
        in_specs=[pl.BlockSpec(memory_space=pltpu.SMEM), vmem, vmem, pl.BlockSpec(memory_space=pltpu.HBM)],
        out_specs=vmem,
        scratch_shapes=[
            pltpu.VMEM((n_src * QUAD, 3 * tok, WIN), BF16),
            pltpu.VMEM((steps, PLANES, QUAD * tok, LANES), F32),
            pltpu.VMEM((steps, PLANES, QUAD * tok, LANES), F32),
            pltpu.VMEM((steps, PLANES, QUAD * tok, LANES), F32),
            pltpu.VMEM((steps, QUAD, tok, LANES), F32),
            pltpu.SemaphoreType.DMA((steps, QUAD)),
            pltpu.SemaphoreType.DMA((steps, QUAD)),
            pltpu.SemaphoreType.DMA((steps, PLANES, CUTS)),
            pltpu.SemaphoreType.DMA((steps, PLANES, CUTS)),
            pltpu.SemaphoreType.DMA((steps, PLANES, CUTS)),
            pltpu.SemaphoreType.DMA((steps, QUAD)),
            pltpu.SemaphoreType.DMA((steps, QUAD)),
            pltpu.VMEM((steps, QUAD, r_tiles, TILE, LANES), BF16),
            pltpu.SemaphoreType.DMA((steps, QUAD)),
        ] + [pltpu.VMEM((QUAD, r_tiles, TILE, LANES), BF16)] * steps,
        compiler_params=pltpu.CompilerParams(collective_id=1, has_side_effects=True, vmem_limit_bytes=56 * 2 ** 20),
        name="collect",
    )(ints, win, tokens, o_rows)


def solution(mesh):
    ep_size = mesh.shape['ep']

    def device_step(tokens, expert_ids, norm_gain, w_router, w_gate, w_up, w_down):
        pairs = expert_ids.shape[0] * expert_ids.shape[1]
        r_max = 3 * pairs // 2
        u_rows, meta, ints = spread(r_max, tokens, expert_ids, norm_gain, w_router)
        u_rows = u_rows.reshape(-1, LANES)
        o_rows, win = experts(ep_size, r_max, ints, meta, u_rows, w_gate, w_up, w_down)
        return collect(ints, win, tokens, o_rows.reshape(-1, r_max // TILE, TILE, LANES))

    row_spec = P(('dp', 'ep'), None)
    expert_spec = P('ep', None, None)
    return jax.shard_map(device_step, mesh=mesh, in_specs=(row_spec, row_spec, P(None), P(None, None), expert_spec, expert_spec, expert_spec), out_specs=row_spec, check_vma=False)
```

profile of v0, /device:TPU:3, one launch (start us, length us, event | category | flops | bytes accessed | tf_op | source)
XLA Modules:
  0.0 230.4 jit_solution(15215277923416057769)
XLA Ops:
  0.0 1.3 reshape.9.gain_ref
  1.3 58.3 %spread.1 = (bf16[16,2048,128]{2,1,0:T(8,128)(2,1)}, f32[16,16,128]{2,1,0:T(8,128)}, s32[64,256]{1,0:T(8,128)}) custom-call(bf16[128,2048]{1,0:T(8,128)(2,1)} %x_ref.3, s32[8,128]{1,0:T(8,128)} %bitcast.5, bf16[1,2048]{1,0:T(2,128)(2,1)} %reshape.9.gain_ref, bf16[2048,128]{1,0:T(8,128)(2,1)} %wr_ref.1), custom_call_target="tpu_custom_call" | custom-call | tf_op jit(solution)/shard_map/spread/pallas_call | solution.py:257
  59.6 46.8 %experts.1 = (bf16[16,1536,128]{2,1,0:T(8,128)(2,1)}, f32[64,8,256]{2,1,0:T(8,128)}) custom-call(s32[64,256]{1,0:T(8,128)} %get-tuple-element.10.ints, f32[16,16,128]{2,1,0:T(8,128)} %get-tuple-element.11.meta, bf16[32768,128]{1,0:T(8,128)(2,1)} %bitcast.3, bf16[8,2048,768]{2,1,0:T(8,128)(2,1)} %w1_hbm.1, bf16[8,2048,768]{2,1,0:T(8,128)(2,1)} %w3_hbm.1, ...), custom_call_target="tpu_custom_call" | custom-call | tf_op jit(solution)/shard_map/experts/pallas_call | solution.py:440
  106.4 122.1 %collect.1 = bf16[128,2048]{1,0:T(8,128)(2,1)} custom-call(s32[64,256]{1,0:T(8,128)} %get-tuple-element.10.ints, f32[64,8,256]{2,1,0:T(8,128)} %get-tuple-element.13.win, bf16[128,2048]{1,0:T(8,128)(2,1)} %x_ref.3, bf16[16,96,16,128]{3,2,1,0:T(8,128)(2,1)} %bitcast.4), custom_call_target="tpu_custom_call" | custom-call | tf_op jit(solution)/shard_map/collect/pallas_call | solution.py:627
  228.5 1.9 copy.9
where the time goes:
time: 232 us; the launch traced here: 230 us
  Pallas kernels  227 us (98%)
  local copies, waits for them, and re-layouts  3.17 us (1%)
    pallas_call x1, Pallas kernels, collect(): pl.pallas_call(functools.partial(collect_kernel, n_src, steps), out_shape...  122 us
    pallas_call x1, Pallas kernels, spread(): pl.pallas_call(functools.partial(spread_kernel, r_max), out_shape=(jax.Sh...  58.3 us
    pallas_call x1, Pallas kernels, experts(): pl.pallas_call(functools.partial(expert_kernel, n_src, sub, r_max), out_s...  46.8 us

commit v1 on v0

--- a/solution.py
+++ b/solution.py
@@ -11,7 +11,7 @@
 LANES = 128
 BM = 128
 WIN = 256
-CUTS = 1
+CUTS = 2
 TILE = 16
 PITCH = 17
 STEP = 8
@@ -69,18 +69,23 @@
         rows = pl.ds(h * half, half)
         return pltpu.make_async_copy(u_all.at[b, rows], u_hbm.at[b, rows], out_sem.at[b, h])
 
-    for h in range(2):
-        @pl.when(z < PLANES - 1)
-        def _():
-            hop(me, h, 0).start()
-
-        @pl.when(z > 0)
-        def _():
-            hop(me, h, 1).start()
-
-        hop(me, h, 2).start()
-        hop(me, h, 3).start()
-        out_copy(me, h).start()
+    def own_sends():
+        for h in range(2):
+            @pl.when(z < PLANES - 1)
+            def _():
+                hop(me, h, 0).start()
+
+            @pl.when(z > 0)
+            def _():
+                hop(me, h, 1).start()
+
+            hop(me, h, 2).start()
+            hop(me, h, 3).start()
+            out_copy(me, h).start()
+
+    @pl.when(c == 0)
+    def _():
+        own_sends()
 
     logits = jnp.dot(ub[...], wr_ref[...], preferred_element_type=F32)
     top = jnp.max(logits, axis=1, keepdims=True)
@@ -104,6 +109,10 @@
     pos_s[...] = jnp.where(hit, base + rank, -1.0)
     t_id = iota((tok, LANES), 0).astype(F32)
     lane_f = lane.astype(F32)
+
+    @pl.when(c == 1)
+    def _():
+        own_sends()
 
     def pack(zd, _):
         for m in range(QUAD):
@@ -507,10 +516,15 @@
     def quad_wait(k, m):
         remote(stage.at[k, m], rows[k].at[m], send_q.at[k, m], recv_q.at[k, m], z * QUAD + m).wait_recv()
 
-    for k in range(steps):
-        for m in others:
-            stage_copy(k, m).wait()
-            quad_copy(k, m).start()
+    def quad_sends():
+        for k in range(steps):
+            for m in others:
+                stage_copy(k, m).wait()
+                quad_copy(k, m).start()
+
+    @pl.when(c == 0)
+    def _():
+        quad_sends()
 
     row_id = iota((tok, WIN), 0).astype(F32)
 
@@ -523,12 +537,36 @@
 
     lax.fori_loop(0, n_src * QUAD, build, 0)
 
+    @pl.when(c == 1)
+    def _():
+        quad_sends()
+
+    def right(k, zd, h, n):
+        rows_h = pl.ds(h * (plane // n), plane // n)
+        return remote(part.at[k, zd, rows_h], from_l.at[k, zd, rows_h], send_z.at[k, zd, h], recv_l.at[k, zd, h], me + QUAD)
+
+    def left(k, zd, h, n):
+        rows_h = pl.ds(h * (plane // n), plane // n)
+        return remote(part.at[k, zd, rows_h], from_r.at[k, zd, rows_h], send_z.at[k, zd, h], recv_r.at[k, zd, h], me - QUAD)
+
+    def cut(k, farthest, body):
+        if k == 0 and farthest:
+            @pl.when(c == 0)
+            def _():
+                body(1)
+
+            @pl.when(c == 1)
+            def _():
+                body(2)
+        else:
+            body(1)
+
     def combine(k):
         own_copy(k).wait()
         for m in others:
             quad_wait(k, m)
 
-        def token_block(s, _):
+        def token_block(s):
             acc = jnp.zeros((3 * tok, LANES), F32)
             for m in range(QUAD):
                 start = ints[48 + s, z * QUAD + m]
@@ -536,53 +574,80 @@
                 acc += jnp.dot(mix[s * QUAD + m], span, preferred_element_type=F32)
             part[k, s // QUAD, pl.ds(pl.multiple_of(lax.rem(s, QUAD) * tok, tok), tok), :] = acc[0:tok] + acc[tok:2 * tok] + acc[2 * tok:]
 
+        def one_plane(i, _):
+            zd = (PLANES - 1 - i) * (1 - z // 2) + i * (z // 2)
+
+            def one_block(m, _):
+                token_block(zd * QUAD + m)
+                return 0
+
+            lax.fori_loop(0, QUAD, one_block, 0)
+
+            for j in range(PLANES - 1):
+                @pl.when(i == j)
+                def _():
+                    def to_right(n):
+                        for h in range(n):
+                            right(k, PLANES - 1 - j, h, n).start()
+
+                    def to_left(n):
+                        for h in range(n):
+                            left(k, j, h, n).start()
+
+                    @pl.when(z == 0)
+                    def _():
+                        cut(k, j == 0, to_right)
+
+                    @pl.when(z == PLANES - 1)
+                    def _():
+                        cut(k, j == 0, to_left)
+
             return 0
 
-        lax.fori_loop(0, n_src, token_block, 0)
-
-    bit = plane // CUTS
-
-    def right(k, zd, h):
-        part_h = pl.ds(h * bit, bit)
-        return remote(part.at[k, zd, part_h], from_l.at[k, zd, part_h], send_z.at[k, zd, h], recv_l.at[k, zd, h], me + QUAD)
-
-    def left(k, zd, h):
-        part_h = pl.ds(h * bit, bit)
-        return remote(part.at[k, zd, part_h], from_r.at[k, zd, part_h], send_z.at[k, zd, h], recv_r.at[k, zd, h], me - QUAD)
+        lax.fori_loop(0, PLANES, one_plane, 0)
 
     def forward(k):
-        for i, h in [(i, h) for i in range(PLANES - 1) for h in range(CUTS)]:
+        for i in range(PLANES - 1):
             for to_right in (True, False):
                 zd = PLANES - 1 - i if to_right else i
                 box = from_l if to_right else from_r
                 go = right if to_right else left
-                rows_h = pl.ds(h * bit, bit)
+
+                def relay(n):
+                    for h in range(n):
+                        rows_h = pl.ds(h * (plane // n), plane // n)
+                        go(k, zd, h, n).wait_recv()
+                        part[k, zd, rows_h] += box[k, zd, rows_h]
+                        go(k, zd, h, n).start()
 
                 @pl.when(z < zd if to_right else z > zd)
                 def _():
                     @pl.when(z > 0 if to_right else z < PLANES - 1)
                     def _():
-                        go(k, zd, h).wait_recv()
-                        part[k, zd, rows_h] += box[k, zd, rows_h]
-
-                    go(k, zd, h).start()
+                        cut(k, i == 0, relay)
 
     def final_copy(k, m):
         src = part.at[k, z, pl.ds(m * tok, tok)]
         return remote(src, fin.at[k, q], send_f.at[k, m], recv_f.at[k, q], z * QUAD + m)
 
     def finish(k):
-        @pl.when(z > 0)
-        def _():
-            for h in range(CUTS):
-                right(k, z, h).wait_recv()
-            part[k, z] += from_l[k, z]
-
-        @pl.when(z < PLANES - 1)
-        def _():
-            for h in range(CUTS):
-                left(k, z, h).wait_recv()
-            part[k, z] += from_r[k, z]
+        for zd in range(PLANES):
+            @pl.when(z == zd)
+            def _():
+                def from_left(n):
+                    for h in range(n):
+                        right(k, zd, h, n).wait_recv()
+
+                def from_right(n):
+                    for h in range(n):
+                        left(k, zd, h, n).wait_recv()
+
+                if zd > 0:
+                    cut(k, zd == PLANES - 1, from_left)
+                    part[k, zd] += from_l[k, zd]
+                if zd < PLANES - 1:
+                    cut(k, zd == 0, from_right)
+                    part[k, zd] += from_r[k, zd]
 
         for m in others:
             final_copy(k, m).start()
@@ -609,13 +674,19 @@
         for zd in range(PLANES):
             @pl.when(z < zd)
             def _():
-                for h in range(CUTS):
-                    right(k, zd, h).wait_send()
+                def done(n):
+                    for h in range(n):
+                        right(k, zd, h, n).wait_send()
+
+                cut(k, zd == PLANES - 1, done)
 
             @pl.when(z > zd)
             def _():
-                for h in range(CUTS):
-                    left(k, zd, h).wait_send()
+                def done(n):
+                    for h in range(n):
+                        left(k, zd, h, n).wait_send()
+
+                cut(k, zd == 0, done)
 
 
 def collect(ints, win, tokens, o_rows):

time: 232 us -> 232 us (level)
  the two profiles are of different devices: /device:TPU:3 before, /device:TPU:0 now
where the time goes in v1:
time: 232 us; the launch traced here: 235 us
  Pallas kernels  232 us (100%)
  local copies, waits for them, and re-layouts  3.17 us (1%)
    pallas_call x1, Pallas kernels, collect(): pl.pallas_call(functools.partial(collect_kernel, n_src, steps), out_shape...  128 us
    pallas_call x1, Pallas kernels, spread(): pl.pallas_call(functools.partial(spread_kernel, r_max), out_shape=(jax.Sh...  59.9 us
    pallas_call x1, Pallas kernels, experts(): pl.pallas_call(functools.partial(expert_kernel, n_src, sub, r_max), out_s...  43.7 us

profile of v1, /device:TPU:0, one launch (start us, length us, event | category | flops | bytes accessed | tf_op | source)
XLA Modules:
  0.0 234.7 jit_solution(8787250619060405526)
XLA Ops:
  0.0 1.3 reshape.9.gain_ref
  1.3 59.9 %spread.1 = (bf16[16,2048,128]{2,1,0:T(8,128)(2,1)}, f32[16,16,128]{2,1,0:T(8,128)}, s32[64,256]{1,0:T(8,128)}) custom-call(bf16[128,2048]{1,0:T(8,128)(2,1)} %x_ref.3, s32[8,128]{1,0:T(8,128)} %bitcast.5, bf16[1,2048]{1,0:T(2,128)(2,1)} %reshape.9.gain_ref, bf16[2048,128]{1,0:T(8,128)(2,1)} %wr_ref.1), custom_call_target="tpu_custom_call" | custom-call | tf_op jit(solution)/shard_map/spread/pallas_call | solution.py:266
  61.2 43.7 %experts.1 = (bf16[16,1536,128]{2,1,0:T(8,128)(2,1)}, f32[64,8,256]{2,1,0:T(8,128)}) custom-call(s32[64,256]{1,0:T(8,128)} %get-tuple-element.10.ints, f32[16,16,128]{2,1,0:T(8,128)} %get-tuple-element.11.meta, bf16[32768,128]{1,0:T(8,128)(2,1)} %bitcast.3, bf16[8,2048,768]{2,1,0:T(8,128)(2,1)} %w1_hbm.1, bf16[8,2048,768]{2,1,0:T(8,128)(2,1)} %w3_hbm.1, ...), custom_call_target="tpu_custom_call" | custom-call | tf_op jit(solution)/shard_map/experts/pallas_call | solution.py:449
  104.9 127.9 %collect.1 = bf16[128,2048]{1,0:T(8,128)(2,1)} custom-call(s32[64,256]{1,0:T(8,128)} %get-tuple-element.10.ints, f32[64,8,256]{2,1,0:T(8,128)} %get-tuple-element.13.win, bf16[128,2048]{1,0:T(8,128)(2,1)} %x_ref.3, bf16[16,96,16,128]{3,2,1,0:T(8,128)(2,1)} %bitcast.4), custom_call_target="tpu_custom_call" | custom-call | tf_op jit(solution)/shard_map/collect/pallas_call | solution.py:698
  232.8 1.9 copy.9

commit v2 on v1

--- a/solution.py
+++ b/solution.py
@@ -211,7 +211,7 @@
     group = (iota((LANES, LANES), 0) // e_loc == iota((LANES, LANES), 1)).astype(F32).astype(BF16)
     n_rows = jnp.dot(cnt.astype(BF16), group, preferred_element_type=F32)
     ints[0:16, LANES:] = jnp.zeros((16, LANES), jnp.int32)
-    ints[0:16, :LANES] = meta[:, pl.ds(q, 1), :].reshape(n_dev, LANES).astype(jnp.int32)
+    ints[0:16, :LANES] = (meta[:, pl.ds(q, 1), :].reshape(n_dev, LANES).astype(jnp.int32) + iota((n_dev, LANES), 0) * tok) * sub
     ints[16:32, :LANES] = cnt.astype(jnp.int32)
     run = jnp.zeros((1, LANES), F32)
     for s in range(n_dev):
@@ -344,12 +344,11 @@
     def expert(e, _):
         slot = lax.rem(e, 2)
         def take(s, j0, n, i, at):
-            t = s * LANES + ints[s, j0 + i]
-            src = u_vm[pl.ds(pl.multiple_of(t * sub, sub), sub), :]
-            xf[pl.ds(at * PITCH, sub), :] = src.astype(F32)
+            src = u_vm[pl.ds(pl.multiple_of(ints[s, j0 + i], sub), sub), :]
+            xf[pl.ds(at, sub), :] = src.astype(F32)
 
         def give(s, j0, n, i, at):
-            o_all[pl.ds(at * PITCH, sub), :] = xf[pl.ds((n + i) * PITCH, sub), :]
+            o_all[pl.ds(at, sub), :] = xf[pl.ds(n + i * PITCH, sub), :]
 
         def sweep(body, target, spare):
             n = jnp.int32(0)
@@ -359,10 +358,10 @@
                 cnt = ints[16 + s, lane0 + e]
                 to = target(s, n)
                 for i in range(STEP):
-                    at = to + i if target is by_row else jnp.where(i < cnt, to + i, spare)
+                    at = to + i * PITCH if target is by_row else jnp.where(i < cnt, to + i * PITCH, spare)
                     body(s, pre[s], n, i, at)
                 starts.append(n)
-                n = n + cnt
+                n = n + cnt * PITCH
                 top = jnp.maximum(top, cnt)
             for s in range(n_src):
                 cnt = ints[16 + s, lane0 + e]
@@ -371,7 +370,7 @@
                 def _():
                     to = target(s, starts[s])
                     for i in range(STEP, STEP + MORE):
-                        body(s, pre[s], starts[s], i, jnp.where(i < cnt, to + i, spare))
+                        body(s, pre[s], starts[s], i, jnp.where(i < cnt, to + i * PITCH, spare))
 
             @pl.when(top > STEP + MORE)
             def _():
@@ -379,11 +378,11 @@
                     cnt = ints[16 + s, lane0 + e]
 
                     def row(i, _):
-                        body(s, pre[s], n, i, target(s, n) + i)
+                        body(s, pre[s], n, i, target(s, n) + i * PITCH)
                         return 0
 
                     lax.fori_loop(STEP + MORE, cnt, row, 0)
-                    return n + cnt
+                    return n + cnt * PITCH
 
                 lax.fori_loop(0, n_src, source, jnp.int32(0))
 
@@ -393,9 +392,9 @@
             return n
 
         def by_slot(s, n):
-            return ints[32 + s, me] + pre[s]
-
-        n = sweep(take, by_row, r_max + 2 * STEP)
+            return (ints[32 + s, me] + pre[s]) * PITCH
+
+        n = sweep(take, by_row, (r_max + 2 * STEP) * PITCH)
 
         for w in load(e, (0, 1, 2)):
             w.wait()
@@ -413,9 +412,9 @@
                     xf[pl.ds(r0 + k * 4 + j, BM, stride=PITCH), :] = o[:, j * LANES:(j + 1) * LANES]
             return 0
 
-        lax.fori_loop(0, (n + BM - 1) // BM, block, 0)
-
-        sweep(give, by_slot, r_max)
+        lax.fori_loop(0, (n + BM * PITCH - 1) // (BM * PITCH), block, 0)
+
+        sweep(give, by_slot, r_max * PITCH)
         for s in range(n_src):
             pre[s] = pre[s] + ints[16 + s, lane0 + e]
 
@@ -606,25 +605,30 @@
 
         lax.fori_loop(0, PLANES, one_plane, 0)
 
-    def forward(k):
-        for i in range(PLANES - 1):
-            for to_right in (True, False):
-                zd = PLANES - 1 - i if to_right else i
-                box = from_l if to_right else from_r
-                go = right if to_right else left
-
-                def relay(n):
-                    for h in range(n):
-                        rows_h = pl.ds(h * (plane // n), plane // n)
-                        go(k, zd, h, n).wait_recv()
-                        part[k, zd, rows_h] += box[k, zd, rows_h]
-                        go(k, zd, h, n).start()
-
-                @pl.when(z < zd if to_right else z > zd)
-                def _():
-                    @pl.when(z > 0 if to_right else z < PLANES - 1)
-                    def _():
-                        cut(k, i == 0, relay)
+    def relay(k, at, zd, to_right):
+        box = from_l if to_right else from_r
+        go = right if to_right else left
+
+        def body(n):
+            for h in range(n):
+                rows_h = pl.ds(h * (plane // n), plane // n)
+                go(k, zd, h, n).wait_recv()
+                part[k, zd, rows_h] += box[k, zd, rows_h]
+                go(k, zd, h, n).start()
+
+        @pl.when(z == at)
+        def _():
+            cut(k, zd == (PLANES - 1 if to_right else 0), body)
+
+    def forward_first(k):
+        relay(k, 1, 3, True)
+        relay(k, 2, 0, False)
+
+    def forward_rest(k):
+        relay(k, 1, 2, True)
+        relay(k, 2, 1, False)
+        relay(k, 1, 0, False)
+        relay(k, 2, 3, True)
 
     def final_copy(k, m):
         src = part.at[k, z, pl.ds(m * tok, tok)]
@@ -655,9 +659,12 @@
 
     for k in range(steps):
         combine(k)
-        forward(k)
+        if k > 0:
+            forward_rest(k - 1)
+        forward_first(k)
         if k > 0:
             finish(k - 1)
+    forward_rest(steps - 1)
     finish(steps - 1)
 
     for k in range(steps):

time: 232 us -> 220 us (0.948); the launches traced: 235 us -> 218 us
  Pallas kernels: 232 us -> 215 us
    pallas_call x1, Pallas kernels: 128 us -> 100 us  [collect(): pl.pallas_call(functools.partial(collect_kernel, n_src, steps), out_shape...]
    pallas_call x1, Pallas kernels: 43.7 us -> 55 us  [experts(): pl.pallas_call(functools.partial(expert_kernel, n_src, sub, r_max), out_s...]
where the time goes in v2:
time: 220 us; the launch traced here: 218 us
  Pallas kernels  215 us (98%)
  local copies, waits for them, and re-layouts  3.17 us (1%)
    pallas_call x1, Pallas kernels, collect(): pl.pallas_call(functools.partial(collect_kernel, n_src, steps), out_shape...  100 us
    pallas_call x1, Pallas kernels, spread(): pl.pallas_call(functools.partial(spread_kernel, r_max), out_shape=(jax.Sh...  59.9 us
    pallas_call x1, Pallas kernels, experts(): pl.pallas_call(functools.partial(expert_kernel, n_src, sub, r_max), out_s...  55 us

profile of v2, /device:TPU:0, one launch (start us, length us, event | category | flops | bytes accessed | tf_op | source)
XLA Modules:
  0.0 218.2 jit_solution(13917657191128719610)
XLA Ops:
  0.0 1.3 reshape.9.gain_ref
  1.3 59.9 %spread.1 = (bf16[16,2048,128]{2,1,0:T(8,128)(2,1)}, f32[16,16,128]{2,1,0:T(8,128)}, s32[64,256]{1,0:T(8,128)}) custom-call(bf16[128,2048]{1,0:T(8,128)(2,1)} %x_ref.3, s32[8,128]{1,0:T(8,128)} %bitcast.5, bf16[1,2048]{1,0:T(2,128)(2,1)} %reshape.9.gain_ref, bf16[2048,128]{1,0:T(8,128)(2,1)} %wr_ref.1), custom_call_target="tpu_custom_call" | custom-call | tf_op jit(solution)/shard_map/spread/pallas_call | solution.py:266
  61.2 55.0 %experts.1 = (bf16[16,1536,128]{2,1,0:T(8,128)(2,1)}, f32[64,8,256]{2,1,0:T(8,128)}) custom-call(s32[64,256]{1,0:T(8,128)} %get-tuple-element.10.ints, f32[16,16,128]{2,1,0:T(8,128)} %get-tuple-element.11.meta, bf16[32768,128]{1,0:T(8,128)(2,1)} %bitcast.3, bf16[8,2048,768]{2,1,0:T(8,128)(2,1)} %w1_hbm.1, bf16[8,2048,768]{2,1,0:T(8,128)(2,1)} %w3_hbm.1, ...), custom_call_target="tpu_custom_call" | custom-call | tf_op jit(solution)/shard_map/experts/pallas_call | solution.py:448
  116.2 100.1 %collect.1 = bf16[128,2048]{1,0:T(8,128)(2,1)} custom-call(s32[64,256]{1,0:T(8,128)} %get-tuple-element.10.ints, f32[64,8,256]{2,1,0:T(8,128)} %get-tuple-element.13.win, bf16[128,2048]{1,0:T(8,128)(2,1)} %x_ref.3, bf16[16,96,16,128]{3,2,1,0:T(8,128)(2,1)} %bitcast.4), custom_call_target="tpu_custom_call" | custom-call | tf_op jit(solution)/shard_map/collect/pallas_call | solution.py:705
  216.3 1.9 copy.9

commit v3 on v2

--- a/solution.py
+++ b/solution.py
@@ -83,9 +83,7 @@
             hop(me, h, 3).start()
             out_copy(me, h).start()
 
-    @pl.when(c == 0)
-    def _():
-        own_sends()
+    own_sends()
 
     logits = jnp.dot(ub[...], wr_ref[...], preferred_element_type=F32)
     top = jnp.max(logits, axis=1, keepdims=True)
@@ -109,10 +107,6 @@
     pos_s[...] = jnp.where(hit, base + rank, -1.0)
     t_id = iota((tok, LANES), 0).astype(F32)
     lane_f = lane.astype(F32)
-
-    @pl.when(c == 1)
-    def _():
-        own_sends()
 
     def pack(zd, _):
         for m in range(QUAD):
@@ -372,7 +366,12 @@
                     for i in range(STEP, STEP + MORE):
                         body(s, pre[s], starts[s], i, jnp.where(i < cnt, to + i * PITCH, spare))
 
-            @pl.when(top > STEP + MORE)
+                    @pl.when(cnt > STEP + MORE)
+                    def _():
+                        for i in range(STEP + MORE, STEP + 2 * MORE):
+                            body(s, pre[s], starts[s], i, jnp.where(i < cnt, to + i * PITCH, spare))
+
+            @pl.when(top > STEP + 2 * MORE)
             def _():
                 def source(s, n):
                     cnt = ints[16 + s, lane0 + e]
@@ -381,7 +380,7 @@
                         body(s, pre[s], n, i, target(s, n) + i * PITCH)
                         return 0
 
-                    lax.fori_loop(STEP + MORE, cnt, row, 0)
+                    lax.fori_loop(STEP + 2 * MORE, cnt, row, 0)
                     return n + cnt * PITCH
 
                 lax.fori_loop(0, n_src, source, jnp.int32(0))

time: 220 us -> 215 us (0.977)
  Pallas kernels: 215 us -> 210 us
    pallas_call x1, Pallas kernels: 55 us -> 40.3 us  [experts(): pl.pallas_call(functools.partial(expert_kernel, n_src, sub, r_max), out_s...]
    pallas_call x1, Pallas kernels: 100 us -> 111 us  [collect(): pl.pallas_call(functools.partial(collect_kernel, n_src, steps), out_shape...]
where the time goes in v3:
time: 215 us; the launch traced here: 214 us
  Pallas kernels  210 us (98%)
  local copies, waits for them, and re-layouts  3.17 us (1%)
    pallas_call x1, Pallas kernels, collect(): pl.pallas_call(functools.partial(collect_kernel, n_src, steps), out_shape...  111 us
    pallas_call x1, Pallas kernels, spread(): pl.pallas_call(functools.partial(spread_kernel, r_max), out_shape=(jax.Sh...  59.4 us
    pallas_call x1, Pallas kernels, experts(): pl.pallas_call(functools.partial(expert_kernel, n_src, sub, r_max), out_s...  40.3 us

profile of v3, /device:TPU:0, one launch (start us, length us, event | category | flops | bytes accessed | tf_op | source)
XLA Modules:
  0.0 213.5 jit_solution(3191102484430690570)
XLA Ops:
  0.0 1.3 reshape.9.gain_ref
  1.3 59.4 %spread.1 = (bf16[16,2048,128]{2,1,0:T(8,128)(2,1)}, f32[16,16,128]{2,1,0:T(8,128)}, s32[64,256]{1,0:T(8,128)}) custom-call(bf16[128,2048]{1,0:T(8,128)(2,1)} %x_ref.3, s32[8,128]{1,0:T(8,128)} %bitcast.5, bf16[1,2048]{1,0:T(2,128)(2,1)} %reshape.9.gain_ref, bf16[2048,128]{1,0:T(8,128)(2,1)} %wr_ref.1), custom_call_target="tpu_custom_call" | custom-call | tf_op jit(solution)/shard_map/spread/pallas_call | solution.py:260
  60.7 40.3 %experts.1 = (bf16[16,1536,128]{2,1,0:T(8,128)(2,1)}, f32[64,8,256]{2,1,0:T(8,128)}) custom-call(s32[64,256]{1,0:T(8,128)} %get-tuple-element.10.ints, f32[16,16,128]{2,1,0:T(8,128)} %get-tuple-element.11.meta, bf16[32768,128]{1,0:T(8,128)(2,1)} %bitcast.3, bf16[8,2048,768]{2,1,0:T(8,128)(2,1)} %w1_hbm.1, bf16[8,2048,768]{2,1,0:T(8,128)(2,1)} %w3_hbm.1, ...), custom_call_target="tpu_custom_call" | custom-call | tf_op jit(solution)/shard_map/experts/pallas_call | solution.py:447
  101.0 110.7 %collect.1 = bf16[128,2048]{1,0:T(8,128)(2,1)} custom-call(s32[64,256]{1,0:T(8,128)} %get-tuple-element.10.ints, f32[64,8,256]{2,1,0:T(8,128)} %get-tuple-element.13.win, bf16[128,2048]{1,0:T(8,128)(2,1)} %x_ref.3, bf16[16,96,16,128]{3,2,1,0:T(8,128)(2,1)} %bitcast.4), custom_call_target="tpu_custom_call" | custom-call | tf_op jit(solution)/shard_map/collect/pallas_call | solution.py:704
  211.6 1.9 copy.9

commit v4 on v3

--- a/solution.py
+++ b/solution.py
@@ -129,11 +129,6 @@
     def route_copy(d):
         return remote(packet.at[d // QUAD], meta.at[me], send_m.at[d], recv_m.at[me], d)
 
-    for d in range(n_dev):
-        @pl.when(d != me)
-        def _():
-            route_copy(d).start()
-
     meta[me] = packet[z]
 
     def take(b, h, ways):
@@ -187,6 +182,11 @@
     step_z(2)
     step_y(1)
     step_z(3)
+    for d in range(n_dev):
+        @pl.when(d != me)
+        def _():
+            route_copy(d).start()
+
     step_y(2)
     step_y(3)
     for b in range(n_dev):

time: 215 us -> 217 us (level)
  Pallas kernels: 210 us -> 214 us
    pallas_call x1, Pallas kernels: 111 us -> 114 us  [collect(): pl.pallas_call(functools.partial(collect_kernel, n_src, steps), out_shape...]
where the time goes in v4:
time: 217 us
  Pallas kernels  214 us (99%)
  local copies, waits for them, and re-layouts  3.17 us (1%)
    pallas_call x1, Pallas kernels, collect(): pl.pallas_call(functools.partial(collect_kernel, n_src, steps), out_shape...  114 us
    pallas_call x1, Pallas kernels, spread(): pl.pallas_call(functools.partial(spread_kernel, r_max), out_shape=(jax.Sh...  59.6 us
    pallas_call x1, Pallas kernels, experts(): pl.pallas_call(functools.partial(expert_kernel, n_src, sub, r_max), out_s...  40.5 us

profile of v4, /device:TPU:0, one launch (start us, length us, event | category | flops | bytes accessed | tf_op | source)
XLA Modules:
  0.0 217.4 jit_solution(2914108006794302835)
XLA Ops:
  0.0 1.3 reshape.9.gain_ref
  1.3 59.6 %spread.1 = (bf16[16,2048,128]{2,1,0:T(8,128)(2,1)}, f32[16,16,128]{2,1,0:T(8,128)}, s32[64,256]{1,0:T(8,128)}) custom-call(bf16[128,2048]{1,0:T(8,128)(2,1)} %x_ref.3, s32[8,128]{1,0:T(8,128)} %bitcast.5, bf16[1,2048]{1,0:T(2,128)(2,1)} %reshape.9.gain_ref, bf16[2048,128]{1,0:T(8,128)(2,1)} %wr_ref.1), custom_call_target="tpu_custom_call" | custom-call | tf_op jit(solution)/shard_map/spread/pallas_call | solution.py:260
  60.9 40.5 %experts.1 = (bf16[16,1536,128]{2,1,0:T(8,128)(2,1)}, f32[64,8,256]{2,1,0:T(8,128)}) custom-call(s32[64,256]{1,0:T(8,128)} %get-tuple-element.10.ints, f32[16,16,128]{2,1,0:T(8,128)} %get-tuple-element.11.meta, bf16[32768,128]{1,0:T(8,128)(2,1)} %bitcast.3, bf16[8,2048,768]{2,1,0:T(8,128)(2,1)} %w1_hbm.1, bf16[8,2048,768]{2,1,0:T(8,128)(2,1)} %w3_hbm.1, ...), custom_call_target="tpu_custom_call" | custom-call | tf_op jit(solution)/shard_map/experts/pallas_call | solution.py:447
  101.4 114.1 %collect.1 = bf16[128,2048]{1,0:T(8,128)(2,1)} custom-call(s32[64,256]{1,0:T(8,128)} %get-tuple-element.10.ints, f32[64,8,256]{2,1,0:T(8,128)} %get-tuple-element.13.win, bf16[128,2048]{1,0:T(8,128)(2,1)} %x_ref.3, bf16[16,96,16,128]{3,2,1,0:T(8,128)(2,1)} %bitcast.4), custom_call_target="tpu_custom_call" | custom-call | tf_op jit(solution)/shard_map/collect/pallas_call | solution.py:704
  215.5 1.9 copy.9
